TPU v7x, 512 devices: a whole 4x8x8 slice. The times are simulated.
512 devices in a mesh: row: 16 (over z, core), col: 32 (over y, x).
Axes of the slice: x: 4, y: 8, z: 8, core: 2. Of those that a mesh axis runs over, the one named last changes fastest.
Arguments:
- ainv: float32 [4, 2048, 2, 4096], P(None, 'row', None, 'col'), may hold values from -6 to 6
- lhat_first: float32 [4, 2048, 512], P(None, ('row', 'col')), may hold values from -0.078125 to 0.078125
- lhat_second: float32 [4, 2048, 512], P(None, ('row', 'col')), may hold values from -0.09375 to 0.09375
- second_on_first: float32 [512, 512], replicated, may hold values from -0.25 to 0.25
- dinv_first: float32 [512, 512], P(None, 'col'), may hold values from -6 to 6
- dinv_second: float32 [512, 512], P(None, 'col'), may hold values from -6 to 6
- anc_first: int32 [48], replicated, may hold values from 0 to 63, as said below
- anc_second: int32 [32], replicated, may hold values from 0 to 63, as said below
Outputs:
- cross_first: float32 [4, 2048, 512], P(None, 'row', 'col')
- diag_first: float32 [512, 512], P(None, 'col')
- cross_second: float32 [4, 2048, 512], P(None, 'row', 'col')
- link_second: float32 [512, 512], P(None, 'col')
- diag_second: float32 [512, 512], P(None, 'col')
Inputs may be any that keep to these rules, and one draw needn't show every extreme that they name: `anc_first`: 48 different tile numbers in increasing order. `anc_second`: 32 different tile numbers in increasing order, each also listed in anc_first.
All inputs are finite; a program needn't handle non-finite values.
Results may differ from a plain program's by a relative error of at most 0.000088.
Values sent between devices are 32-bit elements; how exact they have to be, the bound alone decides.
A program may use at most 64 MiB of HBM per device.

v0:
```python
import functools

import jax
import jax.numpy as jnp
from jax import lax
from jax.experimental import pallas as pl
from jax.experimental.pallas import tpu as pltpu
from jax.sharding import PartitionSpec as P

MESH = pl.DeviceIdType.MESH
F32 = jnp.float32
BF16 = jnp.bfloat16
X, Y, Z = 4, 8, 8
NR, NC = 16, 32


class Phases:
    def __init__(self):
        self.scope = None

    def __call__(self, name):
        if self.scope is not None:
            self.scope.__exit__(None, None, None)
        self.scope = None
        if name:
            self.scope = jax.named_scope(name)
            self.scope.__enter__()


def split(value):
    high = value.astype(BF16)
    return high, (value - high.astype(F32)).astype(BF16)


def mm(left, right):
    return jnp.dot(left, right, preferred_element_type=F32)


def mm3(high, low, both):
    rows, half = high.shape[0], both.shape[1] // 2
    out = mm(jnp.concatenate([high, low], axis=0), both)
    return out[:rows, :half] + (out[rows:, :half] + out[:rows, half:])


def kernel(
    a_hbm, s_hbm, l1_hbm, l2_hbm, d1_hbm, d2_hbm, anc1_hbm, anc2_hbm,
    cross1_ref, diag1_ref, cross2_ref, link_ref, diag2_ref,
    abuf, a_high, a_low, sbuf, s_both, l1_ref, l2_ref, d1_ref, d2_ref, anc1_ref, anc2_ref,
    rbuf, r_both, own, pieces, mbuf, m_both, part_sum, pt, cr,
    ts, tr, ls, lr, r0, tg, tsum, gb, lsum, xt, lk,
    local_sem, a_send, a_recv, my_send, my_recv, mx_send, mx_recv, sc_send, sc_recv,
    qx_send, qx_recv, qy_send, qy_recv, ag_send, ag_recv, dd_send, dd_recv, rs_send, rs_recv, t_send, t_recv, l_send, l_recv,
    tg_send, tg_recv, g_send, g_recv, b_send, b_recv,
):
    phase = Phases()
    phase("p00_greet")
    r, c = lax.axis_index("row"), lax.axis_index("col")
    z, core = r // 2, r % 2
    y, x = c // X, c % X
    right, left, across = (x + 1) % X, (x + X - 1) % X, (x + 2) % X
    base_y = (z + Z - 2 * (y % 4)) % Z
    to_row = 2 * ((2 * (r // 4) + y) % Z) + x // 2
    to_self = jnp.logical_and(to_row == r, y % 4 == r // 4)

    def remote(src, dst, send, recv, row, col):
        return pltpu.make_async_remote_copy(
            src_ref=src, dst_ref=dst, send_sem=send, recv_sem=recv,
            device_id=(row, col), device_id_type=MESH,
        )

    def came(part, recv):
        remote(part, part, l_send, recv, r, c).wait_recv()

    def left_here(part, send):
        remote(part, part, send, l_recv, r, c).wait_send()

    local = [
        pltpu.make_async_copy(src, dst, local_sem.at[i])
        for i, (src, dst) in enumerate(
            [
                (l1_hbm, l1_ref), (l2_hbm, l2_ref), (anc1_hbm, anc1_ref), (anc2_hbm, anc2_ref),
                (s_hbm, sbuf), (a_hbm, abuf.at[x]), (d1_hbm, d1_ref), (d2_hbm, d2_ref),
            ]
        )
    ]
    for copy in local:
        copy.start()

    barrier = pltpu.get_barrier_semaphore()

    def greet(row, col):
        pl.semaphore_signal(barrier, inc=1, device_id=(row, col), device_id_type=MESH)

    for xq in range(4):
        for par in range(2):
            from_row, from_col = (y % 4) * X + xq, 4 * base_y + 2 * core + par

            @pl.when(jnp.logical_not(jnp.logical_and(from_row == r, from_col == c)))
            def _():
                greet(from_row, from_col)

    greet(r, y * X + right)
    greet(r, y * X + left)
    greet(r, y * X + across)
    for d in range(1, Y):
        greet(r, (y + d) % Y * X + x)

    def greet_row(d, carry):
        greet((r + d) % NR, c)
        return carry

    lax.fori_loop(1, NR, greet_row, 0)

    phase("p01_rows")
    nat = lax.broadcasted_iota(jnp.int32, (512, 1), 0)
    target = (nat // 16 % 4) * 128 + (nat // 64) * 16 + nat % 16
    ones = jnp.where(lax.broadcasted_iota(jnp.int32, (512, 512), 1) == target, 1.0, 0.0).astype(BF16)

    def moved(value):
        out = mm(jnp.concatenate(split(value), axis=0), ones)
        return out[:16] + out[16:]

    tile_ids = lax.broadcasted_iota(jnp.int32, (4, 1), 0) * NR + r

    def keeps(anc_ref):
        hits = jnp.where(anc_ref[...] == tile_ids, 1.0, 0.0).astype(F32)
        return jnp.max(hits, axis=1, keepdims=True)

    for copy in local[0:4]:
        copy.wait()
    keep1, keep2 = keeps(anc1_ref), keeps(anc2_ref)
    rows1 = [l1_ref[a] * keep1[a : a + 1] for a in range(4)]
    rows2 = [l2_ref[a] * keep2[a : a + 1] for a in range(4)]
    m1 = jnp.concatenate(rows1, axis=0)
    m1_moved = moved(m1)

    phase("p02_n2")
    local[4].wait()
    sh, sl = split(sbuf[...])
    s_both[:, 0:512] = sh
    s_both[:, 512:1024] = sl
    n2 = jnp.concatenate(rows2, axis=0) - mm3(*split(m1), s_both[...])
    n2_moved = moved(n2)
    for a in range(4):
        yh, s = a % 2, a // 2
        for k in range(4):
            lanes = slice(k * 128, (k + 1) * 128)
            own[yh * 4 + k, s, pl.ds(0, 4, stride=2), :] = m1_moved[a * 4 : a * 4 + 4, lanes]
            own[yh * 4 + k, s, pl.ds(1, 4, stride=2), :] = n2_moved[a * 4 : a * 4 + 4, lanes]
            rbuf[0, a, y, x, pl.ds(k, 4, stride=4), :] = n2[a * 4 : a * 4 + 4, lanes]
            rbuf[1, a, y, x, pl.ds(k, 4, stride=4), :] = rows1[a][:, lanes]

    for copy in local[5:]:
        copy.wait()
    phase("p03_barrier")
    pl.semaphore_wait(barrier, 3 + 7 + 15 + 8 - to_self.astype(jnp.int32))

    phase("p04_send")
    slot = (r % X) * 2 + x % 2
    for yh in range(2):
        for k in range(4):
            to_col = (r // X + 4 * yh) * X + k
            here = jnp.logical_and(to_row == r, c == to_col)
            copy = remote(own.at[yh * 4 + k], pieces.at[slot], sc_send, sc_recv, to_row, to_col)

            @pl.when(jnp.logical_not(here))
            def _():
                copy.start()

            @pl.when(here)
            def _():
                pieces[slot] = own[yh * 4 + k]

    def a_move(at, half, to, recv):
        part = abuf.at[at, pl.ds(half * 512, 512)]
        remote(part, part, a_send, a_recv.at[recv], r, y * X + to).start()

    a_move(x, 0, right, 0)
    a_move(x, 1, left, 1)
    for to in (right, left, across):
        part = rbuf.at[1, 3, y, x]
        remote(part, part, qx_send, qx_recv, r, y * X + to).start()
    a_move(x, 1, right, 2)
    a_move(x, 0, left, 2)

    parts = (4, 3)

    def r_send(w):
        for d in (4, 3, 5, 2, 6, 1, 7):
            part = rbuf.at[w, 0 : parts[w], y, x]
            remote(part, part, my_send.at[w], my_recv.at[w], r, (y + d) % Y * X + x).start()

    def r_part(w, at, half):
        return rbuf.at[w, 0 : parts[w], half * 4 : half * 4 + 4, at]

    def r_move(w, at, half, to, recv):
        part = r_part(w, at, half)
        remote(part, part, mx_send, mx_recv.at[w, recv], r, y * X + to).start()

    def quarter_over_y():
        came(rbuf.at[1, 3, y, 0:3], qx_recv)
        for d in (4, 3, 5, 2, 6, 1, 7):
            part = rbuf.at[1, 3, y]
            remote(part, part, qy_send, qy_recv, r, (y + d) % Y * X + x).start()

    def r_spread(w):
        came(rbuf.at[w, 0 : parts[w], 0:7, x], my_recv.at[w])
        r_move(w, x, 0, right, 0)
        r_move(w, x, 1, left, 1)
        r_move(w, x, 1, right, 2)
        r_move(w, x, 0, left, 2)

    def r_forward(w):
        came(r_part(w, left, 0), mx_recv.at[w, 0])
        r_move(w, left, 0, right, 2)
        came(r_part(w, right, 1), mx_recv.at[w, 1])
        r_move(w, right, 1, left, 2)

    def r_finish(w):
        came(rbuf.at[w, 0 : parts[w], :, 0:2], mx_recv.at[w, 2])
        if w == 1:
            came(rbuf.at[1, 3, 0:7], qy_recv)
        flat = rbuf.at[w].reshape(2048, 128)
        for k in range(4):
            high, low = split(flat[pl.ds(k, 512, stride=4), :])
            r_both[w, k, :, 0:128] = high
            r_both[w, k, :, 128:256] = low

    r_send(0)
    r_send(1)

    phase("p05_scwait")

    @pl.when(to_self)
    def _():
        came(own.at[0:7], sc_recv)

    @pl.when(jnp.logical_not(to_self))
    def _():
        came(own, sc_recv)

    def pair(zs, cs):
        return 2 * ((zs + Z - 2 * (y % 4)) % Z) + cs

    own_pair = pair(z, core)
    for xq in range(4):
        for s in range(2):
            for m in range(2):
                both = [pieces[2 * xq + par, s, pl.ds(m, 4, stride=2), :] for par in range(2)]
                mbuf[m, xq, s, own_pair] = jnp.concatenate(both, axis=0)

    def slab(m, at):
        return mbuf.at[m, :, :, at]

    def to_partner(m, at):
        remote(slab(m, at), slab(m, at), dd_send, dd_recv.at[m], r + 1 - 2 * core, c).start()

    phase("p06_agsend")
    for m in range(2):
        for d in (4, 3, 5, 2, 6, 1, 7):
            to = (z + d) % Z * 2 + core
            part = slab(m, own_pair)
            remote(part, part, ag_send, ag_recv.at[m, z], to, c).start()
        to_partner(m, own_pair)

    phase("p07_await")
    came(abuf.at[left, pl.ds(0, 512)], a_recv.at[0])
    a_move(left, 0, right, 3)
    came(abuf.at[right, pl.ds(512, 512)], a_recv.at[1])
    a_move(right, 1, left, 3)

    phase("p08_n2y")
    r_spread(0)
    quarter_over_y()

    def gathered(m):
        for d in (7, 1, 6, 2, 5, 3, 4):
            zs = (z + d) % Z
            came(slab(m, pair(zs, core)), ag_recv.at[m, zs])
            to_partner(m, pair(zs, core))

    def columns(m):
        came(mbuf.at[m, :, :, 0:8], dd_recv.at[m])
        for xq in range(4):
            for s in range(2):
                high, low = split(mbuf[m, xq, s].reshape(128, 128))
                m_both[m, xq, s * 128 : (s + 1) * 128, 0:128] = high
                m_both[m, xq, s * 128 : (s + 1) * 128, 128:256] = low

    phase("p09_ag0")
    gathered(0)
    phase("p10_dd0")
    columns(0)

    def owner_send(m):
        for d in (4, 3, 5, 2, 6, 1, 7):
            to = (y + d) % Y
            part = pt.at[:, m, pl.ds(pl.multiple_of(to * 16, 16), 16)]
            remote(part, cr.at[m, y], rs_send, rs_recv.at[m], r, to * X + x).start()

    def slot_product(rb, at, m, fresh):
        rows = pl.ds(pl.multiple_of(rb * 128, 128), 128)
        if fresh:
            both = [abuf[at, pl.ds(rb * 256 + s, 128, stride=2), :] for s in range(2)]
            high, low = split(jnp.concatenate(both, axis=1))
            a_high[at, rows] = high
            a_low[at, rows] = low
        else:
            high, low = a_high[at, rows], a_low[at, rows]
        out = mm(high, m_both[m, at])
        return out[:, 0:128] + (out[:, 128:256] + mm(low, m_both[m, at, :, 0:128]))

    def multiply_near(rb, carry):
        total = slot_product(rb, x, 0, True)
        for at in (left, right):
            total = total + slot_product(rb, at, 0, True)
        part_sum[rb] = total
        return carry

    def multiply_across(rb, carry):
        pt[rb, 0] = (part_sum[rb] + slot_product(rb, across, 0, True)).T
        return carry

    def multiply_second(rb, carry):
        total = slot_product(rb, 0, 1, False)
        for at in range(1, X):
            total = total + slot_product(rb, at, 1, False)
        pt[rb, 1] = total.T
        return carry

    phase("p11_anear")
    came(abuf.at[0], a_recv.at[2])
    phase("p12_mmnear")
    lax.fori_loop(0, 4, multiply_near, 0, unroll=True)
    phase("p13_across")
    came(abuf.at[across], a_recv.at[3])
    phase("p13_mm0")
    lax.fori_loop(0, 4, multiply_across, 0, unroll=True)
    owner_send(0)
    phase("p14_ag1")
    gathered(1)
    phase("p14_n2fwd")
    r_forward(0)
    phase("p14_m1y")
    r_spread(1)
    phase("p15_dd1")
    columns(1)
    phase("p16_mm1")
    lax.fori_loop(0, 4, multiply_second, 0, unroll=True)
    owner_send(1)
    r0_full = mm3(*split(d1_ref[...]), s_both[...])
    for k in range(4):
        r0[k] = r0_full[:, k * 128 : (k + 1) * 128]
    phase("p18_n2x")
    r_finish(0)
    def owned(m, keep, out_ref):
        came(cr.at[m, 0:7], rs_recv.at[m])
        mine = pl.ds(pl.multiple_of(y * 16, 16), 16)
        sums = []
        for a in range(4):
            total = pt[a, m, mine]
            for d in range(1, 8):
                total = total + cr[m, (y + d) % Y, a]
            total = -keep[a : a + 1] * total
            out_ref[a] = total
            sums.append(total)
        return split(jnp.concatenate(sums, axis=1))

    def wide(high, low, w, k):
        return mm3(high, low, r_both[w, k])

    phase("p20_c1wait")
    c_high, c_low = owned(0, keep1, cross1_ref)
    phase("p21_link")
    for k in range(4):
        ls[k] = -wide(c_high, c_low, 0, k)

    def link_row(q):
        return NR - 1 - q

    q_own = NR - 1 - r
    collects = q_own < 4

    def send_link(q, carry):
        copy = remote(ls.at[q], lr.at[r], l_send, l_recv, link_row(q), c)

        @pl.when(r != link_row(q))
        def _():
            copy.start()

        return carry

    lax.fori_loop(0, 4, send_link, 0)

    own_tile = z
    holds = core == 1

    def send_sums():
        def send(tile, carry):
            to = 2 * tile + 1
            copy = remote(ts.at[:, tile], tr.at[:, r], t_send, t_recv, to, c)

            @pl.when(to != r)
            def _():
                copy.start()

            return carry

        lax.fori_loop(0, 8, send, 0)

    def send_totals():
        tr[:, r] = ts[:, own_tile]
        came(tr.at[:, 0:15], t_recv)
        total = tr[:, 0]
        for src in range(1, NR):
            total = total + tr[:, src]
        tg[:, own_tile] = total
        tsum[...] = total

        def send(d, carry):
            remote(tsum, tg.at[:, own_tile], tg_send, tg_recv, (r + d) % NR, c).start()
            return carry

        lax.fori_loop(1, NR, send, 0)

    def totals(w):
        return [
            jnp.concatenate([tg[w, 2 * k], tg[w, 2 * k + 1]], axis=0) for k in range(4)
        ]

    phase("p22_m1fwd")
    r_forward(1)
    phase("p24_link")

    @pl.when(collects)
    def _():
        lr[r] = ls[q_own]
        came(lr.at[0:15], l_recv)
        total = lr[0]
        for src in range(1, NR):
            total = total + lr[src]
        lsum[...] = total - r0[q_own]
        for j in range(8):
            to_col = 8 * q_own + j
            copy = remote(lsum, gb.at[c], g_send, g_recv, r, to_col)

            @pl.when(to_col != c)
            def _():
                copy.start()

    phase("p25_c2wait")
    c2_high, c2_low = owned(1, keep2, cross2_ref)
    by_n2 = [wide(c2_high, c2_low, 0, k) for k in range(4)]
    phase("p26_m1x")
    r_finish(1)
    phase("p26_q3")
    high = jnp.concatenate([c_high, c2_high], axis=0)
    low = jnp.concatenate([c_low, c2_low], axis=0)
    by_m1 = [wide(high, low, 1, k) for k in range(4)]
    rest = mm3(*split(jnp.concatenate([part[16:32] for part in by_m1], axis=1)), s_both[...])
    for k in range(4):
        sums = by_n2[k] + rest[:, k * 128 : (k + 1) * 128]
        for half in range(2):
            ts[0, k * 2 + half] = by_m1[k][half * 8 : half * 8 + 8]
            ts[1, k * 2 + half] = sums[half * 8 : half * 8 + 8]

    send_sums()

    root_row = link_row(c // 8)
    is_root = r == root_row

    def link_out():
        gb[c] = lsum[...]
        came(gb.at[0:31], g_recv)
        for k in range(4):
            xt[k] = gb[8 * k : 8 * k + 8].reshape(128, 128).T
        for k in range(4):
            lk[:, k * 128 : (k + 1) * 128] = xt[k, pl.ds(pl.multiple_of(16 * (c % 8), 16), 16), :]

        def send_on(d, carry):
            remote(lk, lk, b_send, b_recv, (r + d) % NR, c).start()
            return carry

        lax.fori_loop(1, NR, send_on, 0)

    phase("p27_twait")

    pl.when(holds)(send_totals)

    phase("p28_root")
    pl.when(is_root)(link_out)
    phase("p29_tgwait")

    @pl.when(holds)
    def _():
        came(tg.at[:, 0:7], tg_recv)

    @pl.when(jnp.logical_not(holds))
    def _():
        came(tg, tg_recv)

    for k, sums in enumerate(totals(0)):
        lanes = slice(k * 128, (k + 1) * 128)
        diag1_ref[:, lanes] = d1_ref[:, lanes] - sums
    sums2 = totals(1)

    phase("p30_lkwait")

    @pl.when(jnp.logical_not(is_root))
    def _():
        came(lk, b_recv)

    phase("p31_tail")
    link = lk[...]
    link_ref[...] = link
    tail = mm3(*split(link), s_both[...])
    for k in range(4):
        lanes = slice(k * 128, (k + 1) * 128)
        diag2_ref[:, lanes] = d2_ref[:, lanes] - (sums2[k] + tail[:, lanes])

    phase("p32_drain")
    left_here(abuf.at[0:3], a_send)
    left_here(rbuf.at[0, :, 0:7, 0], my_send.at[0])
    left_here(rbuf.at[1, 0:3, 0:7, 0], my_send.at[1])
    left_here(rbuf.at[:, 0:3, 0:7], mx_send)
    left_here(rbuf.at[1, 3, 0, 0:3], qx_send)
    left_here(rbuf.at[1, 3, 0:7], qy_send)
    left_here(mbuf.at[:, :, :, 0:7], ag_send)
    left_here(mbuf.at[:, :, :, 0:8], dd_send)
    left_here(cr.at[:, 0:7], rs_send)

    @pl.when(holds)
    def _():
        left_here(tr.at[:, 0:7], t_send)
        left_here(tr.at[:, 0:15], tg_send)

    @pl.when(jnp.logical_not(holds))
    def _():
        left_here(tr.at[:, 0:8], t_send)


    @pl.when(to_self)
    def _():
        left_here(own.at[0:7], sc_send)

    @pl.when(jnp.logical_not(to_self))
    def _():
        left_here(own, sc_send)

    @pl.when(collects)
    def _():
        left_here(lr.at[0:3], l_send)

        @pl.when(is_root)
        def _():
            left_here(gb.at[0:7], g_send)

        @pl.when(jnp.logical_not(is_root))
        def _():
            left_here(gb.at[0:8], g_send)

    @pl.when(jnp.logical_not(collects))
    def _():
        left_here(lr.at[0:4], l_send)

    @pl.when(is_root)
    def _():
        left_here(mbuf.at[0, :, :, 0:15], b_send)

    phase(None)


def hand_out(*refs):
    sems = refs[10]
    copies = [pltpu.make_async_copy(refs[i], refs[5 + i], sems.at[i]) for i in range(5)]
    for copy in copies:
        copy.start()
    for copy in copies:
        copy.wait()


def body(
    ainv, lhat_first, lhat_second, second_on_first, dinv_first, dinv_second, anc_first, anc_second
):
    vmem = pl.BlockSpec(memory_space=pltpu.VMEM)
    hbm = pl.BlockSpec(memory_space=pl.ANY)
    dma = pltpu.SemaphoreType.DMA
    cross = jax.ShapeDtypeStruct((4, 16, 128), F32)
    panel = jax.ShapeDtypeStruct((16, 512), F32)
    found = pl.pallas_call(
        kernel,
        out_shape=tuple(pltpu.VMEM(leaf.shape, F32) for leaf in (cross, panel, cross, panel, panel)),
        in_specs=[hbm] * 8,
        out_specs=(vmem,) * 5,
        scratch_shapes=[
            pltpu.VMEM((4, 1024, 128), F32),
            pltpu.VMEM((4, 512, 256), BF16),
            pltpu.VMEM((4, 512, 256), BF16),
            pltpu.VMEM((512, 512), F32),
            pltpu.VMEM((512, 1024), BF16),
            pltpu.VMEM((4, 4, 512), F32),
            pltpu.VMEM((4, 4, 512), F32),
            pltpu.VMEM((16, 512), F32),
            pltpu.VMEM((16, 512), F32),
            pltpu.VMEM((1, anc_first.shape[0]), jnp.int32),
            pltpu.VMEM((1, anc_second.shape[0]), jnp.int32),
            pltpu.VMEM((2, 4, 8, 4, 16, 128), F32),
            pltpu.VMEM((2, 4, 512, 256), BF16),
            pltpu.VMEM((8, 2, 8, 128), F32),
            pltpu.VMEM((8, 2, 8, 128), F32),
            pltpu.VMEM((2, 4, 2, 16, 8, 128), F32),
            pltpu.VMEM((2, 4, 256, 256), BF16),
            pltpu.VMEM((4, 128, 128), F32),
            pltpu.VMEM((4, 2, 128, 128), F32),
            pltpu.VMEM((2, 8, 4, 16, 128), F32),
            pltpu.VMEM((2, 8, 8, 128), F32),
            pltpu.VMEM((2, 16, 8, 128), F32),
            pltpu.VMEM((4, 16, 128), F32),
            pltpu.VMEM((16, 16, 128), F32),
            pltpu.VMEM((4, 16, 128), F32),
            pltpu.VMEM((2, 8, 8, 128), F32),
            pltpu.VMEM((2, 8, 128), F32),
            pltpu.VMEM((32, 16, 128), F32),
            pltpu.VMEM((16, 128), F32),
            pltpu.VMEM((4, 128, 128), F32),
            pltpu.VMEM((16, 512), F32),
            dma((8,)),
            dma, dma((4,)),
            dma((2,)), dma((2,)),
            dma, dma((2, 3)),
            dma, dma,
            dma, dma,
            dma, dma,
            dma, dma((2, 8)),
            dma, dma((2,)),
            dma, dma((2,)),
            dma, dma,
            dma, dma,
            dma, dma,
            dma, dma,
            dma, dma,
        ],
        compiler_params=pltpu.CompilerParams(collective_id=0, has_side_effects=True),
    )(
        ainv.reshape(1024, 128), second_on_first, lhat_first, lhat_second,
        dinv_first.T, dinv_second.T, anc_first.reshape(1, -1), anc_second.reshape(1, -1),
    )
    cross1, diag1, cross2, link, diag2 = pl.pallas_call(
        hand_out,
        out_shape=(cross, panel, cross, panel, panel),
        in_specs=[vmem] * 5,
        out_specs=(hbm,) * 5,
        scratch_shapes=[dma((5,))],
    )(*[pltpu.with_memory_space_constraint(leaf, pltpu.VMEM) for leaf in found])
    return (
        cross1.transpose(0, 2, 1), diag1.T, cross2.transpose(0, 2, 1), link.T, diag2.T,
    )


def solution(mesh):
    return jax.shard_map(
        body,
        mesh=mesh,
        in_specs=(
            P(None, "row", None, "col"),
            P(None, ("row", "col"), None),
            P(None, ("row", "col"), None),
            P(),
            P(None, "col"),
            P(None, "col"),
            P(),
            P(),
        ),
        out_specs=(
            P(None, "row", "col"),
            P(None, "col"),
            P(None, "row", "col"),
            P(None, "col"),
            P(None, "col"),
        ),
        check_vma=False,
    )
```

profile of v0, /device:TPU:1, one launch (start us, length us, event | category | flops | bytes accessed | tf_op | source)
XLA Modules:
  0.0 64.6 jit_solution(10923651033830540078)
XLA Ops:
  0.6 63.2 %shard_map.119 = (f32[4,16,128]{2,1,0:T(8,128)S(1)}, f32[16,512]{1,0:T(8,128)S(1)}, f32[4,16,128]{2,1,0:T(8,128)S(1)}, f32[16,512]{1,0:T(8,128)S(1)}, f32[16,512]{1,0:T(8,128)S(1)}) custom-call(f32[1024,128]{1,0:T(8,128)} %bitcast.10, f32[512,512]{1,0:T(8,128)} %s_hbm.1, f32[4,4,512]{2,1,0:T(4,128)} %l1_hbm.1, f32[4,4,512]{2,1,0:T(4,128)} %l2_hbm.1, ...), custom_call_target="tpu_custom_call" | custom-call | tf_op jit(solution)/shard_map/pallas_call | solution.py:590
  63.9 0.7 %shard_map.120 = (f32[4,16,128]{2,1,0:T(8,128)}, f32[16,512]{1,0:T(8,128)}, f32[4,16,128]{2,1,0:T(8,128)}, f32[16,512]{1,0:T(8,128)}, f32[16,512]{1,0:T(8,128)}) custom-call(f32[4,16,128]{2,1,0:T(8,128)S(1)} %get-tuple-element.15.refs_0_, f32[16,512]{1,0:T(8,128)S(1)} %get-tuple-element.16.refs_1_, f32[4,16,128]{2,1,0:T(8,128)S(1)} %get-tuple-element.17.refs_2_, ...), custom_call_target="tpu_custom_call" | custom-call | tf_op jit(solution)/shard_map/pallas_call | solution.py:648
where the time goes:
time: 64.7 us; the launch traced here: 64.6 us
  Pallas kernels  63.9 us (99%)
    pallas_call x1, Pallas kernels, body(): pl.pallas_call(kernel, out_shape=tuple((pltpu.VMEM(leaf.shape, F32) for l...  63.2 us

commit v1 on v0

--- a/solution.py
+++ b/solution.py
@@ -79,7 +79,7 @@
         for i, (src, dst) in enumerate(
             [
                 (l1_hbm, l1_ref), (l2_hbm, l2_ref), (anc1_hbm, anc1_ref), (anc2_hbm, anc2_ref),
-                (s_hbm, sbuf), (a_hbm, abuf.at[x]), (d1_hbm, d1_ref), (d2_hbm, d2_ref),
+                (a_hbm, abuf.at[x]), (s_hbm, sbuf), (d1_hbm, d1_ref), (d2_hbm, d2_ref),
             ]
         )
     ]
@@ -132,44 +132,45 @@
     rows1 = [l1_ref[a] * keep1[a : a + 1] for a in range(4)]
     rows2 = [l2_ref[a] * keep2[a : a + 1] for a in range(4)]
     m1 = jnp.concatenate(rows1, axis=0)
-    m1_moved = moved(m1)
-
-    phase("p02_n2")
+
+    def lay_own(m, value):
+        for a in range(4):
+            for k in range(4):
+                part = value[a * 4 : a * 4 + 4, k * 128 : (k + 1) * 128]
+                own[m, a % 2 * 4 + k, a // 2 * 4 : a // 2 * 4 + 4] = part
+
+    def lay_rows(w, value):
+        for a in range(4):
+            for k in range(4):
+                part = value[a * 4 : a * 4 + 4, k * 128 : (k + 1) * 128]
+                rbuf[w, a, y, x, pl.ds(k, 4, stride=4), :] = part
+
+    lay_own(0, moved(m1))
+    lay_rows(1, m1)
     local[4].wait()
-    sh, sl = split(sbuf[...])
-    s_both[:, 0:512] = sh
-    s_both[:, 512:1024] = sl
-    n2 = jnp.concatenate(rows2, axis=0) - mm3(*split(m1), s_both[...])
-    n2_moved = moved(n2)
-    for a in range(4):
-        yh, s = a % 2, a // 2
-        for k in range(4):
-            lanes = slice(k * 128, (k + 1) * 128)
-            own[yh * 4 + k, s, pl.ds(0, 4, stride=2), :] = m1_moved[a * 4 : a * 4 + 4, lanes]
-            own[yh * 4 + k, s, pl.ds(1, 4, stride=2), :] = n2_moved[a * 4 : a * 4 + 4, lanes]
-            rbuf[0, a, y, x, pl.ds(k, 4, stride=4), :] = n2[a * 4 : a * 4 + 4, lanes]
-            rbuf[1, a, y, x, pl.ds(k, 4, stride=4), :] = rows1[a][:, lanes]
-
-    for copy in local[5:]:
-        copy.wait()
     phase("p03_barrier")
     pl.semaphore_wait(barrier, 3 + 7 + 15 + 8 - to_self.astype(jnp.int32))
 
     phase("p04_send")
     slot = (r % X) * 2 + x % 2
-    for yh in range(2):
-        for k in range(4):
-            to_col = (r // X + 4 * yh) * X + k
-            here = jnp.logical_and(to_row == r, c == to_col)
-            copy = remote(own.at[yh * 4 + k], pieces.at[slot], sc_send, sc_recv, to_row, to_col)
-
-            @pl.when(jnp.logical_not(here))
-            def _():
-                copy.start()
-
-            @pl.when(here)
-            def _():
-                pieces[slot] = own[yh * 4 + k]
+
+    def scatter(m):
+        for yh in range(2):
+            for k in range(4):
+                to_col = (r // X + 4 * yh) * X + k
+                here = jnp.logical_and(to_row == r, c == to_col)
+                part = own.at[m, yh * 4 + k]
+                copy = remote(part, pieces.at[m, slot], sc_send.at[m], sc_recv.at[m], to_row, to_col)
+
+                @pl.when(jnp.logical_not(here))
+                def _():
+                    copy.start()
+
+                @pl.when(here)
+                def _():
+                    pieces[m, slot] = own[m, yh * 4 + k]
+
+    scatter(0)
 
     def a_move(at, half, to, recv):
         part = abuf.at[at, pl.ds(half * 512, 512)]
@@ -182,6 +183,17 @@
         remote(part, part, qx_send, qx_recv, r, y * X + to).start()
     a_move(x, 1, right, 2)
     a_move(x, 0, left, 2)
+
+    phase("p02_n2")
+    for copy in local[5:]:
+        copy.wait()
+    sh, sl = split(sbuf[...])
+    s_both[:, 0:512] = sh
+    s_both[:, 512:1024] = sl
+    n2 = jnp.concatenate(rows2, axis=0) - mm3(*split(m1), s_both[...])
+    lay_own(1, moved(n2))
+    lay_rows(0, n2)
+    scatter(1)
 
     parts = (4, 3)
 
@@ -229,25 +241,10 @@
     r_send(0)
     r_send(1)
 
-    phase("p05_scwait")
-
-    @pl.when(to_self)
-    def _():
-        came(own.at[0:7], sc_recv)
-
-    @pl.when(jnp.logical_not(to_self))
-    def _():
-        came(own, sc_recv)
-
     def pair(zs, cs):
         return 2 * ((zs + Z - 2 * (y % 4)) % Z) + cs
 
     own_pair = pair(z, core)
-    for xq in range(4):
-        for s in range(2):
-            for m in range(2):
-                both = [pieces[2 * xq + par, s, pl.ds(m, 4, stride=2), :] for par in range(2)]
-                mbuf[m, xq, s, own_pair] = jnp.concatenate(both, axis=0)
 
     def slab(m, at):
         return mbuf.at[m, :, :, at]
@@ -255,13 +252,29 @@
     def to_partner(m, at):
         remote(slab(m, at), slab(m, at), dd_send, dd_recv.at[m], r + 1 - 2 * core, c).start()
 
-    phase("p06_agsend")
-    for m in range(2):
+    def along_z(m):
+        @pl.when(to_self)
+        def _():
+            came(own.at[m, 0:7], sc_recv.at[m])
+
+        @pl.when(jnp.logical_not(to_self))
+        def _():
+            came(own.at[m], sc_recv.at[m])
+
+        for xq in range(4):
+            for s in range(2):
+                both = [pieces[m, 2 * xq + par, s * 4 : s * 4 + 4] for par in range(2)]
+                mbuf[m, xq, s, own_pair] = jnp.concatenate(both, axis=0)
         for d in (4, 3, 5, 2, 6, 1, 7):
             to = (z + d) % Z * 2 + core
             part = slab(m, own_pair)
             remote(part, part, ag_send, ag_recv.at[m, z], to, c).start()
         to_partner(m, own_pair)
+
+    phase("p05_sc0")
+    along_z(0)
+    phase("p06_sc1")
+    along_z(1)
 
     phase("p07_await")
     came(abuf.at[left, pl.ds(0, 512)], a_recv.at[0])
@@ -417,11 +430,16 @@
         tg[:, own_tile] = total
         tsum[...] = total
 
-        def send(d, carry):
-            remote(tsum, tg.at[:, own_tile], tg_send, tg_recv, (r + d) % NR, c).start()
+        def send(to, carry):
+            copy = remote(tsum, tg.at[:, own_tile], tg_send, tg_recv, to, c)
+
+            @pl.when(to != r)
+            def _():
+                copy.start()
+
             return carry
 
-        lax.fori_loop(1, NR, send, 0)
+        lax.fori_loop(0, NR, send, 0)
 
     def totals(w):
         return [
@@ -477,11 +495,16 @@
         for k in range(4):
             lk[:, k * 128 : (k + 1) * 128] = xt[k, pl.ds(pl.multiple_of(16 * (c % 8), 16), 16), :]
 
-        def send_on(d, carry):
-            remote(lk, lk, b_send, b_recv, (r + d) % NR, c).start()
+        def send_on(to, carry):
+            copy = remote(lk, lk, b_send, b_recv, to, c)
+
+            @pl.when(to != r)
+            def _():
+                copy.start()
+
             return carry
 
-        lax.fori_loop(1, NR, send_on, 0)
+        lax.fori_loop(0, NR, send_on, 0)
 
     phase("p27_twait")
 
@@ -539,13 +562,15 @@
         left_here(tr.at[:, 0:8], t_send)
 
 
-    @pl.when(to_self)
-    def _():
-        left_here(own.at[0:7], sc_send)
-
-    @pl.when(jnp.logical_not(to_self))
-    def _():
-        left_here(own, sc_send)
+    for m in range(2):
+
+        @pl.when(to_self)
+        def _():
+            left_here(own.at[m, 0:7], sc_send.at[m])
+
+        @pl.when(jnp.logical_not(to_self))
+        def _():
+            left_here(own.at[m], sc_send.at[m])
 
     @pl.when(collects)
     def _():
@@ -606,8 +631,8 @@
             pltpu.VMEM((1, anc_second.shape[0]), jnp.int32),
             pltpu.VMEM((2, 4, 8, 4, 16, 128), F32),
             pltpu.VMEM((2, 4, 512, 256), BF16),
-            pltpu.VMEM((8, 2, 8, 128), F32),
-            pltpu.VMEM((8, 2, 8, 128), F32),
+            pltpu.VMEM((2, 8, 8, 128), F32),
+            pltpu.VMEM((2, 8, 8, 128), F32),
             pltpu.VMEM((2, 4, 2, 16, 8, 128), F32),
             pltpu.VMEM((2, 4, 256, 256), BF16),
             pltpu.VMEM((4, 128, 128), F32),
@@ -628,7 +653,7 @@
             dma, dma((4,)),
             dma((2,)), dma((2,)),
             dma, dma((2, 3)),
-            dma, dma,
+            dma((2,)), dma((2,)),
             dma, dma,
             dma, dma,
             dma, dma((2, 8)),

time: 64.7 us -> 64.1 us (level)
  no operation moved by 1% of the time
where the time goes in v1:
time: 64.1 us; the launch traced here: 63.9 us
  Pallas kernels  63.3 us (99%)
    pallas_call x1, Pallas kernels, body(): pl.pallas_call(kernel, out_shape=tuple((pltpu.VMEM(leaf.shape, F32) for l...  62.6 us

profile of v1, /device:TPU:1, one launch (start us, length us, event | category | flops | bytes accessed | tf_op | source)
XLA Modules:
  0.0 63.9 jit_solution(16953854649025829919)
XLA Ops:
  0.6 62.6 %shard_map.119 = (f32[4,16,128]{2,1,0:T(8,128)S(1)}, f32[16,512]{1,0:T(8,128)S(1)}, f32[4,16,128]{2,1,0:T(8,128)S(1)}, f32[16,512]{1,0:T(8,128)S(1)}, f32[16,512]{1,0:T(8,128)S(1)}) custom-call(f32[1024,128]{1,0:T(8,128)} %bitcast.10, f32[512,512]{1,0:T(8,128)} %s_hbm.1, f32[4,4,512]{2,1,0:T(4,128)} %l1_hbm.1, f32[4,4,512]{2,1,0:T(4,128)} %l2_hbm.1, ...), custom_call_target="tpu_custom_call" | custom-call | tf_op jit(solution)/shard_map/pallas_call | solution.py:615
  63.2 0.7 %shard_map.120 = (f32[4,16,128]{2,1,0:T(8,128)}, f32[16,512]{1,0:T(8,128)}, f32[4,16,128]{2,1,0:T(8,128)}, f32[16,512]{1,0:T(8,128)}, f32[16,512]{1,0:T(8,128)}) custom-call(f32[4,16,128]{2,1,0:T(8,128)S(1)} %get-tuple-element.15.refs_0_, f32[16,512]{1,0:T(8,128)S(1)} %get-tuple-element.16.refs_1_, f32[4,16,128]{2,1,0:T(8,128)S(1)} %get-tuple-element.17.refs_2_, ...), custom_call_target="tpu_custom_call" | custom-call | tf_op jit(solution)/shard_map/pallas_call | solution.py:673

commit v2 on v1

--- a/solution.py
+++ b/solution.py
@@ -389,10 +389,10 @@
         ls[k] = -wide(c_high, c_low, 0, k)
 
     def link_row(q):
-        return NR - 1 - q
-
-    q_own = NR - 1 - r
-    collects = q_own < 4
+        return NR - 1 - 2 * q
+
+    q_own = (NR - 1 - r) // 2
+    collects = jnp.logical_and(core == 1, q_own < 4)
 
     def send_link(q, carry):
         copy = remote(ls.at[q], lr.at[r], l_send, l_recv, link_row(q), c)
@@ -406,11 +406,11 @@
     lax.fori_loop(0, 4, send_link, 0)
 
     own_tile = z
-    holds = core == 1
+    holds = core == 1 - z // 4
 
     def send_sums():
         def send(tile, carry):
-            to = 2 * tile + 1
+            to = 2 * tile + 1 - tile // 4
             copy = remote(ts.at[:, tile], tr.at[:, r], t_send, t_recv, to, c)
 
             @pl.when(to != r)

time: 64.1 us -> 64.9 us (1.012)
  Pallas kernels: 63.3 us -> 64.2 us
    pallas_call x1, Pallas kernels: 62.6 us -> 63.5 us  [body(): pl.pallas_call(kernel, out_shape=tuple((pltpu.VMEM(leaf.shape, F32) for l...]
where the time goes in v2:
time: 64.9 us; the launch traced here: 64.8 us
  Pallas kernels  64.2 us (99%)
    pallas_call x1, Pallas kernels, body(): pl.pallas_call(kernel, out_shape=tuple((pltpu.VMEM(leaf.shape, F32) for l...  63.5 us

profile of v2, /device:TPU:1, one launch (start us, length us, event | category | flops | bytes accessed | tf_op | source)
XLA Modules:
  0.0 64.8 jit_solution(8465786483045771278)
XLA Ops:
  0.6 63.5 %shard_map.119 = (f32[4,16,128]{2,1,0:T(8,128)S(1)}, f32[16,512]{1,0:T(8,128)S(1)}, f32[4,16,128]{2,1,0:T(8,128)S(1)}, f32[16,512]{1,0:T(8,128)S(1)}, f32[16,512]{1,0:T(8,128)S(1)}) custom-call(f32[1024,128]{1,0:T(8,128)} %bitcast.10, f32[512,512]{1,0:T(8,128)} %s_hbm.1, f32[4,4,512]{2,1,0:T(4,128)} %l1_hbm.1, f32[4,4,512]{2,1,0:T(4,128)} %l2_hbm.1, ...), custom_call_target="tpu_custom_call" | custom-call | tf_op jit(solution)/shard_map/pallas_call | solution.py:615
  64.1 0.7 %shard_map.120 = (f32[4,16,128]{2,1,0:T(8,128)}, f32[16,512]{1,0:T(8,128)}, f32[4,16,128]{2,1,0:T(8,128)}, f32[16,512]{1,0:T(8,128)}, f32[16,512]{1,0:T(8,128)}) custom-call(f32[4,16,128]{2,1,0:T(8,128)S(1)} %get-tuple-element.15.refs_0_, f32[16,512]{1,0:T(8,128)S(1)} %get-tuple-element.16.refs_1_, f32[4,16,128]{2,1,0:T(8,128)S(1)} %get-tuple-element.17.refs_2_, ...), custom_call_target="tpu_custom_call" | custom-call | tf_op jit(solution)/shard_map/pallas_call | solution.py:673
